TPU v7x, 32 devices: a whole 2x2x4 slice. The times are simulated.
32 devices in a mesh: dp: 4 (over y, x), tp: 8 (over z, core).
Axes of the slice: x: 2, y: 2, z: 4, core: 2. Of those that a mesh axis runs over, the one named last changes fastest.
Arguments:
- proj_in: bfloat16 [1, 4096, 8192], P(None, 'dp', 'tp'), may hold values from -6 to 6
- kv_grad: bfloat16 [1, 4096, 2048], P(None, ('dp', 'tp')), may hold values from -0.1796875 to 0.1796875
- normed: bfloat16 [1, 4096, 8192], P(None, ('dp', 'tp')), may hold values from -6 to 6
- norm_grad: bfloat16 [1, 4096, 8192], P(None, ('dp', 'tp')), may hold values from -0.6 to 0.6
- first_moment: float32 [1, 8192, 2048], P(None, 'tp', 'dp'), may hold values from -0.6 to 0.6
- second_moment: float32 [1, 8192, 2048], P(None, 'tp', 'dp'), may hold values from 0.002 to 0.02
Outputs:
- new_first: float32 [1, 8192, 2048], P(None, 'tp', 'dp')
- new_second: float32 [1, 8192, 2048], P(None, 'tp', 'dp')
- adam_step: float32 [1, 8192, 2048], P(None, 'tp', 'dp')
- gain_grad: float32 [1, 8192], replicated
All inputs are finite; a program needn't handle non-finite values.
Results may differ from a plain program's by a relative error of at most 0.0003.
Values may be sent and summed in bfloat16 or wider, within the bound.
A program may use at most 128 MiB of HBM per device.

v0:
```python
import jax
import jax.numpy as jnp
from jax import lax
from jax.sharding import PartitionSpec as P

beta_one = 0.9
beta_two = 0.95
correct_one = 0.19
correct_two = 0.0975
epsilon = 1e-08


def adam_update(mean_grad, first_old, second_old):
    new_first = beta_one * first_old + (1.0 - beta_one) * mean_grad
    new_second = beta_two * second_old + (1.0 - beta_two) * mean_grad * mean_grad
    update = new_first / correct_one / (jnp.sqrt(new_second / correct_two) + epsilon)
    return (new_first, new_second, update)


def row_adder(inputs, arrived):
    return lax.dot_general(
        inputs, arrived, (((0,), (0,)), ((), ())), preferred_element_type=jnp.float32
    )


def shards(proj_in, kv_grad, normed, norm_grad, first_moment, second_moment):
    replicas = lax.axis_size("dp")
    local_terms = jnp.sum(norm_grad.astype(jnp.float32) * normed.astype(jnp.float32), axis=1)
    gain_grad = lax.psum(local_terms, ("dp", "tp")) / replicas
    inputs = proj_in[0]
    grad_rows = kv_grad[0]
    local_grad = row_adder(inputs, lax.all_gather(grad_rows, "tp", axis=0, tiled=True))
    mean_grad = lax.psum_scatter(local_grad, "dp", scatter_dimension=1, tiled=True) / replicas
    new_first, new_second, update = adam_update(mean_grad, first_moment[0], second_moment[0])
    firsts = [new_first]
    seconds = [new_second]
    updates = [update]
    return (jnp.stack(firsts), jnp.stack(seconds), jnp.stack(updates), gain_grad)


def solution(mesh):
    return jax.shard_map(
        shards,
        mesh=mesh,
        in_specs=(
            P(None, "dp", "tp"),
            P(None, ("dp", "tp"), None),
            P(None, ("dp", "tp"), None),
            P(None, ("dp", "tp"), None),
            P(None, "tp", "dp"),
            P(None, "tp", "dp"),
        ),
        out_specs=(P(None, "tp", "dp"), P(None, "tp", "dp"), P(None, "tp", "dp"), P()),
        check_vma=False,
    )
```

profile of v0, /device:TPU:0, one launch (start us, length us, event | category | flops | bytes accessed | tf_op | source)
XLA Modules:
  0.0 168.0 jit_solution(9199358891031246904)
XLA Ops:
  7.2 0.0 copy-start
  7.2 0.0 all-gather.3.cloned.1.call-start
  7.2 0.7 all-gather.3.cloned.1.call-update
  7.9 0.0 reduce-scatter.2.cloned.1.call-start
  8.0 51.2 %all-gather.3.cloned.1.call-done = bf16[1,1024,2048]{2,1,0:T(8,128)(2,1)} async-done(((bf16[1,128,2048]{2,1,0:T(8,128)(2,1)}), bf16[1,1024,2048]{2,1,0:T(8,128)(2,1)}) %all-gather.3.cloned.1.call-update) | async-done | bytes 4194320 | tf_op jit(solution)/shard_map/all_gather | solution.py:32
  59.2 0.0 copy-done
  59.2 9.0 %fusion = f32[1024,2048]{1,0:T(8,128)} fusion(bf16[1,1024,2048]{2,1,0:T(8,128)(2,1)} %all-gather.3.cloned.1.call-done, bf16[1,1024,1024]{2,1,0:T(8,128)(2,1)S(1)} %copy-done), kind=kOutput, calls=%fused_computation | convolution fusion | flops 4294967296 | bytes 14680064 | tf_op jit(solution)/shard_map/dot_general | solution.py:21
  68.2 0.0 reduce-scatter.2.cloned.1.call-update
  68.2 2.8 %multiply_reduce_fusion = f32[8192]{0:T(1024)S(1)} fusion(bf16[1,128,8192]{2,1,0:T(8,128)(2,1)} %param.8, bf16[1,128,8192]{2,1,0:T(8,128)(2,1)} %param.9), kind=kLoop, calls=%fused_computation.2 | loop fusion | flops 4186112 | bytes 4227072 | tf_op jit(solution)/shard_map/reduce_sum | solution.py:28
  71.0 40.4 %psum.7 = f32[1,8192]{1,0:T(1,128)S(1)} all-reduce(f32[1,8192]{1,0:T(1,128)S(1)} %bitcast.25), channel_id=1, replica_groups=mesh['dp'=4,'tp'=8] {'dp','tp'}, use_global_device_ids=true, to_apply=%region_2.0 | all-reduce | flops 8192 | bytes 65536 | tf_op jit(solution)/shard_map/psum | solution.py:29
  111.4 0.6 broadcast_multiply_fusion
  112.0 42.7 %reduce-scatter.2.cloned.1.call-done = f32[1024,512]{1,0:T(8,128)} async-done(((f32[1024,2048]{1,0:T(8,128)}), f32[1024,512]{1,0:T(8,128)}) %reduce-scatter.2.cloned.1.call-update) | async-done | bytes 2097168 | tf_op jit(solution)/shard_map/reduce_scatter | solution.py:33
  154.7 6.4 %divide_bitcast_fusion = (f32[1,1024,512]{2,1,0:T(8,128)}, f32[1,1024,512]{2,1,0:T(8,128)}, f32[1,1024,512]{2,1,0:T(8,128)}) fusion(f32[1024,512]{1,0:T(8,128)} %reduce-scatter.2.cloned.1.call-done, f32[1,1024,512]{2,1,0:T(8,128)} %param.10, f32[1,1024,512]{2,1,0:T(8,128)} %param.11), kind=kLoop, calls=%fused_computation.6 | loop fusion | flops 6291456 | bytes 12582912 | tf_op jit(solution)/shard_map/stack | solution.py:38
Async XLA Ops:
  7.2 52.0 %copy-start = (bf16[1,1024,1024]{2,1,0:T(8,128)(2,1)S(1)}, bf16[1,1024,1024]{2,1,0:T(8,128)(2,1)}, u32[]{:S(2)}) copy-start(bf16[1,1024,1024]{2,1,0:T(8,128)(2,1)} %param.6) | copy-start | bytes 6291460
  7.2 52.0 %all-gather.3.cloned.1.call-start = ((), (), s32[]{:S(2)}) async-start(), calls=%async_computation.2 | async-start | bytes 4718592 | tf_op jit(solution)/shard_map/all_gather | solution.py:32
  7.9 146.8 %reduce-scatter.2.cloned.1.call-start = ((), (), s32[]{:S(2)}) async-start(), calls=%async_computation.1 | async-start | bytes 10485760 | tf_op jit(solution)/shard_map/reduce_scatter | solution.py:33
Sparse Core Ops, SparseCore 0:
  9.6 49.5 all-gather.2
  68.3 86.3 reduce-scatter.1
where the time goes:
time: 168 us
  waiting for transfers between devices  94.6 us (56%)
  blocking collectives  40.4 us (24%)
  between operations  14 us (8%)
  other arithmetic  9.91 us (6%)
  matrix products  8.95 us (5%)
    all_gather x1, waiting for transfers between devices, shards(): lax.all_gather(grad_rows, 'tp', axis=0, tiled=True)  51.2 us
    reduce_scatter x1, waiting for transfers between devices, shards(): lax.psum_scatter(local_grad, 'dp', scatter_dimension=1, tiled=True)  42.7 us
    psum x1, blocking collectives, shards(): gain_grad = lax.psum(local_terms, ('dp', 'tp')) / replicas  40.4 us
    dot_general x1, matrix products, row_adder(): lax.dot_general(inputs, arrived, (((0,), (0,)), ((), ())), preferred_elem...  8.95 us
    another operation x1, other arithmetic, shards(): jnp.stack(updates)  6.44 us
  transfers between devices with their start and end apart: 2, of which 2 were waited for; matrix products, arithmetic and copies ran while one was open for 2% of the time, Pallas kernels for 0%

commit v1 on v0

--- a/solution.py
+++ b/solution.py
@@ -26,7 +26,7 @@
 def shards(proj_in, kv_grad, normed, norm_grad, first_moment, second_moment):
     replicas = lax.axis_size("dp")
     local_terms = jnp.sum(norm_grad.astype(jnp.float32) * normed.astype(jnp.float32), axis=1)
-    gain_grad = lax.psum(local_terms, ("dp", "tp")) / replicas
+    gain_grad = jnp.sum(lax.all_gather(local_terms, ("dp", "tp")), axis=0) / replicas
     inputs = proj_in[0]
     grad_rows = kv_grad[0]
     local_grad = row_adder(inputs, lax.all_gather(grad_rows, "tp", axis=0, tiled=True))

time: 168 us -> 217 us (1.29)
  waiting for transfers between devices: 94.6 us -> 182 us
  blocking collectives: 40.4 us -> 0 us
    all_gather x0 -> x1, waiting for transfers between devices: none -> 47.2 us  [shards(): lax.all_gather(local_terms, ('dp', 'tp'))]
    reduce_scatter x1, waiting for transfers between devices: 42.7 us -> 86.2 us  [shards(): lax.psum_scatter(local_grad, 'dp', scatter_dimension=1, tiled=True)]
    psum x1 -> x0, blocking collectives: 40.4 us -> none  [shards(): gain_grad = lax.psum(local_terms, ('dp', 'tp')) / replicas]
    all_gather x1, waiting for transfers between devices: 51.2 us -> 47.7 us  [shards(): lax.all_gather(grad_rows, 'tp', axis=0, tiled=True)]
  transfers between devices with their start and end apart: 2 -> 3, of which waited for: 2 -> 3; matrix products, arithmetic and copies ran while one was open for 2% -> 7% of each run, Pallas kernels for 0% -> 0%
where the time goes in v1:
time: 217 us
  waiting for transfers between devices  182 us (84%)
  between operations  13.8 us (6%)
  other arithmetic  10.6 us (5%)
  matrix products  8.96 us (4%)
    reduce_scatter x1, waiting for transfers between devices, shards(): lax.psum_scatter(local_grad, 'dp', scatter_dimension=1, tiled=True)  86.2 us
    all_gather x1, waiting for transfers between devices, shards(): lax.all_gather(grad_rows, 'tp', axis=0, tiled=True)  47.7 us
    all_gather x1, waiting for transfers between devices, shards(): lax.all_gather(local_terms, ('dp', 'tp'))  47.2 us
    dot_general x1, matrix products, row_adder(): lax.dot_general(inputs, arrived, (((0,), (0,)), ((), ())), preferred_elem...  8.96 us
    another operation x1, other arithmetic, shards(): jnp.stack(updates)  6.44 us
  transfers between devices with their start and end apart: 3, of which 3 were waited for; matrix products, arithmetic and copies ran while one was open for 7% of the time, Pallas kernels for 0%

profile of v1, /device:TPU:0, one launch (start us, length us, event | category | flops | bytes accessed | tf_op | source)
XLA Modules:
  0.0 216.8 jit_solution(10111612424575215444)
XLA Ops:
  7.2 0.0 copy-start
  7.2 0.0 all-gather.5.cloned.1.call-start
  7.2 0.7 all-gather.5.cloned.1.call-update
  7.9 0.0 all-gather.7.cloned.1.call-start
  8.0 3.4 %multiply_reduce_fusion = f32[8192]{0:T(1024)} fusion(bf16[1,128,8192]{2,1,0:T(8,128)(2,1)} %param.8, bf16[1,128,8192]{2,1,0:T(8,128)(2,1)} %param.9), kind=kLoop, calls=%fused_computation.2 | loop fusion | flops 4186112 | bytes 4227072 | tf_op jit(solution)/shard_map/reduce_sum | solution.py:28
  11.4 0.0 all-gather.7.cloned.1.call-update
  11.4 0.0 reduce-scatter.2.cloned.1.call-start
  11.5 47.7 %all-gather.5.cloned.1.call-done = bf16[1,1024,2048]{2,1,0:T(8,128)(2,1)} async-done(((bf16[1,128,2048]{2,1,0:T(8,128)(2,1)}), bf16[1,1024,2048]{2,1,0:T(8,128)(2,1)}) %all-gather.5.cloned.1.call-update) | async-done | bytes 4194320 | tf_op jit(solution)/shard_map/all_gather | solution.py:32
  59.2 0.0 copy-done
  59.2 9.0 %fusion = f32[1024,2048]{1,0:T(8,128)} fusion(bf16[1,1024,2048]{2,1,0:T(8,128)(2,1)} %all-gather.5.cloned.1.call-done, bf16[1,1024,1024]{2,1,0:T(8,128)(2,1)S(1)} %copy-done), kind=kOutput, calls=%fused_computation | convolution fusion | flops 4294967296 | bytes 14680064 | tf_op jit(solution)/shard_map/dot_general | solution.py:21
  68.2 0.0 reduce-scatter.2.cloned.1.call-update
  68.2 47.2 %all-gather.7.cloned.1.call-done = f32[262144]{0:T(1024)} async-done(((f32[8192]{0:T(1024)}), f32[262144]{0:T(1024)}) %all-gather.7.cloned.1.call-update) | async-done | bytes 1048592 | tf_op jit(solution)/shard_map/all_gather | solution.py:29
  115.4 1.4 reshape.26
  116.9 0.1 reduce.2
  117.0 0.6 broadcast_multiply_fusion
  117.6 86.2 %reduce-scatter.2.cloned.1.call-done = f32[1024,512]{1,0:T(8,128)} async-done(((f32[1024,2048]{1,0:T(8,128)}), f32[1024,512]{1,0:T(8,128)}) %reduce-scatter.2.cloned.1.call-update) | async-done | bytes 2097168 | tf_op jit(solution)/shard_map/reduce_scatter | solution.py:33
  203.8 6.4 %divide_bitcast_fusion = (f32[1,1024,512]{2,1,0:T(8,128)}, f32[1,1024,512]{2,1,0:T(8,128)}, f32[1,1024,512]{2,1,0:T(8,128)}) fusion(f32[1024,512]{1,0:T(8,128)} %reduce-scatter.2.cloned.1.call-done, f32[1,1024,512]{2,1,0:T(8,128)} %param.10, f32[1,1024,512]{2,1,0:T(8,128)} %param.11), kind=kLoop, calls=%fused_computation.6 | loop fusion | flops 6291456 | bytes 12582912 | tf_op jit(solution)/shard_map/stack | solution.py:38
Async XLA Ops:
  7.2 52.0 %copy-start = (bf16[1,1024,1024]{2,1,0:T(8,128)(2,1)S(1)}, bf16[1,1024,1024]{2,1,0:T(8,128)(2,1)}, u32[]{:S(2)}) copy-start(bf16[1,1024,1024]{2,1,0:T(8,128)(2,1)} %param.6) | copy-start | bytes 6291460
  7.2 52.0 %all-gather.5.cloned.1.call-start = ((), (), s32[]{:S(2)}) async-start(), calls=%async_computation.2 | async-start | bytes 4718592 | tf_op jit(solution)/shard_map/all_gather | solution.py:32
  7.9 107.5 %all-gather.7.cloned.1.call-start = ((), (), s32[]{:S(2)}) async-start(), calls=%async_computation.3 | async-start | bytes 1081344 | tf_op jit(solution)/shard_map/all_gather | solution.py:29
  11.4 192.4 %reduce-scatter.2.cloned.1.call-start = ((), (), s32[]{:S(2)}) async-start(), calls=%async_computation.1 | async-start | bytes 10485760 | tf_op jit(solution)/shard_map/reduce_scatter | solution.py:33
Sparse Core Ops, SparseCore 0:
  9.6 49.5 all-gather.4
  62.8 52.6 all-gather.6
  118.5 85.2 reduce-scatter.1
